TPU v7x, 32 devices: a whole 2x2x4 slice. The times are simulated.
32 devices in a mesh: batch: 4 (over y, x), ctx: 8 (over z, core).
Axes of the slice: x: 2, y: 2, z: 4, core: 2. Of those that a mesh axis runs over, the one named last changes fastest.
Arguments:
- asked_for: bfloat16 [4, 1024, 64, 64], P('batch', 'ctx'), may hold values from -6 to 6
- offered: bfloat16 [4, 1024, 64, 64], P('batch', 'ctx'), may hold values from -6 to 6
- contents: bfloat16 [4, 1024, 64, 64], P('batch', 'ctx'), may hold values from -6 to 6
- out_weight: bfloat16 [4096, 4096], P('batch'), may hold values from -0.09375 to 0.09375
Outputs:
- layer_out: bfloat16 [4, 1024, 4096], P('batch', 'ctx')
All inputs are finite; a program needn't handle non-finite values.
Results may differ from a plain program's by a relative error of at most 0.006.
Values may be sent and summed in bfloat16 or wider, within the bound.
A program may use at most 128 MiB of HBM per device.

v0:
```python
import jax
import jax.numpy as jnp
from jax import lax
from jax.sharding import PartitionSpec as P


def to_features(values):
    wide = values.astype(jnp.float32)
    return jax.nn.softplus(wide).astype(jnp.bfloat16)


def after_reading(read, count):
    result = read * count**0.5
    return result.astype(jnp.bfloat16)


def look_up(features, state, mass):
    top = jnp.einsum(
        "bthd,bhde->bthe", features, state.astype(jnp.bfloat16), preferred_element_type=jnp.float32
    )
    bottom = jnp.einsum(
        "bthd,bhd->bth", features.astype(jnp.float32), mass, precision=lax.Precision.HIGHEST
    )
    return top / (bottom + 0.001)[..., None]


def shards(asked_for, offered, contents, out_weight):
    query_feature, key_feature = (to_features(asked_for), to_features(offered))
    count = asked_for.shape[1] * lax.axis_size("ctx")
    head_query, head_key, head_value = (
        lax.all_to_all(query_feature, "ctx", split_axis=2, concat_axis=1, tiled=True),
        lax.all_to_all(key_feature, "ctx", split_axis=2, concat_axis=1, tiled=True),
        lax.all_to_all(contents, "ctx", split_axis=2, concat_axis=1, tiled=True),
    )
    state = (
        jnp.einsum("bthd,bthe->bhde", head_key, head_value, preferred_element_type=jnp.float32)
        / count
    )
    mass = jnp.sum(head_key.astype(jnp.float32), axis=1) / count
    head_read = look_up(head_query, state, mass)
    read = lax.all_to_all(head_read, "ctx", split_axis=1, concat_axis=2, tiled=True)
    mixed = after_reading(read, count)
    mixed = mixed.reshape(mixed.shape[0], mixed.shape[1], -1)
    return jnp.einsum(
        "btw,wv->btv",
        mixed,
        lax.all_gather(out_weight, "batch", axis=0, tiled=True),
        preferred_element_type=jnp.float32,
    ).astype(jnp.bfloat16)


def solution(mesh):
    in_specs = (
        P("batch", "ctx", None, None),
        P("batch", "ctx", None, None),
        P("batch", "ctx", None, None),
        P("batch", None),
    )
    out_specs = P("batch", "ctx", None)
    return jax.shard_map(shards, mesh=mesh, in_specs=in_specs, out_specs=out_specs, check_vma=False)
```

profile of v0, /device:TPU:0, one launch (start us, length us, event | category | flops | bytes accessed | tf_op | source)
XLA Modules:
  0.0 329.9 jit_solution(17906474795930241207)
XLA Ops:
  6.5 0.0 all-gather.2.cloned.1.call-start
  6.5 0.7 all-gather.2.cloned.1.call-update
  7.3 0.5 copy-done
  7.8 2.2 fusion.10
  10.0 6.5 %all-to-all-start.2 = ((bf16[1,128,64,64]{1,3,0,2:T(8,128)(2,1)}), bf16[1,128,64,64]{1,3,0,2:T(8,128)(2,1)S(1)}, u32[]{:S(2)}, u32[]{:S(2)}) async-start(bf16[1,128,64,64]{1,3,0,2:T(8,128)(2,1)} %fusion.10), calls=%async_computation.2 | async-start | bytes 2097152 | tf_op jit(solution)/shard_map/all_to_all | solution.py:31
  16.4 0.0 copy-done.1
  16.4 1.2 fusion.9
  17.7 25.3 %all-to-all-done.2 = bf16[1,128,64,64]{1,3,0,2:T(8,128)(2,1)S(1)} async-done(((bf16[1,128,64,64]{1,3,0,2:T(8,128)(2,1)}), bf16[1,128,64,64]{1,3,0,2:T(8,128)(2,1)S(1)}, u32[]{:S(2)}, u32[]{:S(2)}) %all-to-all-start.2) | async-done | bytes 1048608 | tf_op jit(solution)/shard_map/all_to_all | solution.py:31
  43.0 29.0 %all_to_all.54 = bf16[1,128,64,64]{1,3,0,2:T(8,128)(2,1)S(1)} all-to-all(bf16[1,128,64,64]{1,3,0,2:T(8,128)(2,1)S(1)} %fusion.9), channel_id=1, replica_groups=mesh['batch'=4,'ctx'=8] {'ctx'}, dimensions={2} | all-to-all | bytes 2097152 | tf_op jit(solution)/shard_map/all_to_all | solution.py:32
  72.0 3.6 %all-to-all-start.1 = ((bf16[1,128,64,64]{1,3,0,2:T(8,128)(2,1)}), bf16[1,128,64,64]{1,3,0,2:T(8,128)(2,1)S(1)}, u32[]{:S(2)}, u32[]{:S(2)}) async-start(bf16[1,128,64,64]{1,3,0,2:T(8,128)(2,1)} %bitcast.81), calls=%async_computation.1 | async-start | bytes 2097152 | tf_op jit(solution)/shard_map/all_to_all | solution.py:33
  75.5 1.7 copy.48
  77.2 1.5 reshape.53
  78.8 1.7 copy.50
  80.5 2.3 reshape.51
  82.8 19.3 %all-to-all-done.1 = bf16[1,128,64,64]{1,3,0,2:T(8,128)(2,1)S(1)} async-done(((bf16[1,128,64,64]{1,3,0,2:T(8,128)(2,1)}), bf16[1,128,64,64]{1,3,0,2:T(8,128)(2,1)S(1)}, u32[]{:S(2)}, u32[]{:S(2)}) %all-to-all-start.1) | async-done | bytes 1048608 | tf_op jit(solution)/shard_map/all_to_all | solution.py:33
  102.0 1.7 copy.49
  103.7 2.4 reshape.52
  106.1 1.4 convert_reduce_fusion
  107.5 0.5 fusion.15
  108.1 3.2 bitcast_divide_fusion
  111.3 3.9 %copy.35 = f32[1,1024,8,64]{3,2,0,1:T(8,128)} copy(f32[1,1024,8,64]{1,3,2,0:T(8,128)} %bitcast_divide_fusion) | data formatting | bytes 4194304 | tf_op jit(solution)/shard_map/div | solution.py:24
  115.2 5.9 %reshape.56 = f32[8,1,65536]{2,1,0:T(1,128)S(1)} reshape(f32[1024,1,8,64]{3,2,1,0:T(8,128)} %bitcast.69) | data formatting | bytes 4194304
  121.2 52.2 %all_to_all.55 = f32[8,1,65536]{2,1,0:T(1,128)} all-to-all(f32[8,1,65536]{2,1,0:T(1,128)S(1)} %reshape.56), channel_id=1, replica_groups=mesh['batch'=4,'ctx'=8] {'ctx'}, dimensions={0} | all-to-all | bytes 4194304 | tf_op jit(solution)/shard_map/all_to_all | solution.py:41
  173.4 0.5 broadcast.21
  173.9 7.2 %reduce.2 = f32[8,65536]{1,0:T(8,128)S(1)} reduce(f32[8,1,65536]{2,1,0:T(1,128)} %all_to_all.55, f32[]{:T(128)} %broadcast.21), dimensions={1}, to_apply=%all_to_all.49.reduce_sub_computation | reduce | bytes 4194308 | tf_op jit(solution)/shard_map/all_to_all | solution.py:41
  181.1 3.7 %reshape.57 = f32[1024,1,8,64]{3,2,1,0:T(8,128)} reshape(f32[8,65536]{1,0:T(8,128)S(1)} %reduce.2) | data formatting | bytes 4194304
  184.8 2.8 copy.36
  187.6 0.3 multiply_convert_fusion
  187.9 0.3 copy.41
  188.2 0.3 copy.37
  188.4 120.6 %all-gather.2.cloned.1.call-done = bf16[4096,4096]{1,0:T(8,128)(2,1)} async-done(((bf16[1024,4096]{1,0:T(8,128)(2,1)}), bf16[4096,4096]{1,0:T(8,128)(2,1)}) %all-gather.2.cloned.1.call-update) | async-done | bytes 33554448 | tf_op jit(solution)/shard_map/all_gather | solution.py:47
  309.0 14.0 %fusion = bf16[1,128,4096]{2,1,0:T(8,128)(2,1)} fusion(bf16[128,4096]{0,1:T(8,128)(2,1)S(1)} %bitcast.73, bf16[4096,4096]{1,0:T(8,128)(2,1)} %all-gather.2.cloned.1.call-done), kind=kOutput, calls=%fused_computation.3 | convolution fusion | flops 4295491584 | bytes 35651584 | tf_op jit(solution)/shard_map/btw,wv->btv/dot_general | solution.py:44
  (6 shorter events, 0.0 us)
Async XLA Ops:
  6.5 1.2 copy-start
  6.5 302.5 %all-gather.2.cloned.1.call-start = ((), (), s32[]{:S(2)}) async-start(), calls=%async_computation.4 | async-start | bytes 41943040 | tf_op jit(solution)/shard_map/all_gather | solution.py:47
  10.0 6.5 %copy-start.1 = (bf16[1,128,64,64]{1,3,2,0:T(8,128)(2,1)S(1)}, bf16[1,128,64,64]{1,3,2,0:T(8,128)(2,1)}, u32[]{:S(2)}) copy-start(bf16[1,128,64,64]{1,3,2,0:T(8,128)(2,1)} %param.5) | copy-start | bytes 3145732
  10.0 33.0 %all-to-all-start.2 = ((bf16[1,128,64,64]{1,3,0,2:T(8,128)(2,1)}), bf16[1,128,64,64]{1,3,0,2:T(8,128)(2,1)S(1)}, u32[]{:S(2)}, u32[]{:S(2)}) async-start(bf16[1,128,64,64]{1,3,0,2:T(8,128)(2,1)} %fusion.10), calls=%async_computation.2 | async-start | bytes 2097152 | tf_op jit(solution)/shard_map/all_to_all | solution.py:31
  72.0 30.1 %all-to-all-start.1 = ((bf16[1,128,64,64]{1,3,0,2:T(8,128)(2,1)}), bf16[1,128,64,64]{1,3,0,2:T(8,128)(2,1)S(1)}, u32[]{:S(2)}, u32[]{:S(2)}) async-start(bf16[1,128,64,64]{1,3,0,2:T(8,128)(2,1)} %bitcast.81), calls=%async_computation.1 | async-start | bytes 2097152 | tf_op jit(solution)/shard_map/all_to_all | solution.py:33
  103.7 4.3 %copy-start.2 = (bf16[1024,8,64]{0,2,1:T(8,128)(2,1)S(1)}, bf16[1024,8,64]{0,2,1:T(8,128)(2,1)}, u32[]{:S(2)}) copy-start(bf16[1024,8,64]{0,2,1:T(8,128)(2,1)} %reshape.51) | copy-start | bytes 3145732
Sparse Core Ops, SparseCore 0:
  9.2 299.7 all-gather.1
where the time goes:
time: 331 us; the launch traced here: 330 us
  waiting for transfers between devices  166 us (50%)
  blocking collectives  81.2 us (25%)
  local copies, waits for them, and re-layouts  29.2 us (9%)
  matrix products  17.8 us (5%)
  between operations  13.5 us (4%)
  other arithmetic  12.3 us (4%)
  starting transfers between devices  10 us (3%)
    all_gather x1, waiting for transfers between devices, shards(): lax.all_gather(out_weight, 'batch', axis=0, tiled=True)  121 us
    all_to_all x1, blocking collectives, shards(): lax.all_to_all(head_read, 'ctx', split_axis=1, concat_axis=2, tiled=True)  52.2 us
    all_to_all x1, blocking collectives, shards(): lax.all_to_all(key_feature, 'ctx', split_axis=2, concat_axis=1, tiled=True)  29 us
    all_to_all x1, waiting for transfers between devices, shards(): lax.all_to_all(query_feature, 'ctx', split_axis=2, concat_axis=1, tiled=T...  25.3 us
    all_to_all x1, waiting for transfers between devices, shards(): lax.all_to_all(contents, 'ctx', split_axis=2, concat_axis=1, tiled=True)  19.3 us
    dot_general x1, matrix products, shards(): jnp.einsum('btw,wv->btv', mixed, lax.all_gather(out_weight, 'batch', axis...  14 us
    unnamed x9, local copies, waits for them, and re-layouts  10.4 us
    all_to_all x1, other arithmetic, shards(): lax.all_to_all(head_read, 'ctx', split_axis=1, concat_axis=2, tiled=True)  7.22 us
  transfers between devices with their start and end apart: 3, of which 3 were waited for; matrix products, arithmetic and copies ran while one was open for 14% of the time, Pallas kernels for 0%

commit v1 on v0

--- a/solution.py
+++ b/solution.py
@@ -2,6 +2,22 @@
 import jax.numpy as jnp
 from jax import lax
 from jax.sharding import PartitionSpec as P
+
+
+def summed_both_ways(shard, axis, dim, product):
+    length, index, width = (lax.axis_size(axis), lax.axis_index(axis), shard.shape[dim])
+    ahead = [(i, (i + 1) % length) for i in range(length)]
+    backward = [(i, (i - 1) % length) for i in range(length)]
+    middle = length // 2
+    from_left = from_right = shard
+    total = product(shard, index * width)
+    for step in range(1, middle + 1):
+        from_left = lax.ppermute(from_left, axis, ahead)
+        if step < length - middle:
+            from_right = lax.ppermute(from_right, axis, backward)
+            total = total + product(from_right, (index + step) % length * width)
+        total = total + product(from_left, (index - step) % length * width)
+    return total
 
 
 def to_features(values):
@@ -41,11 +57,16 @@
     read = lax.all_to_all(head_read, "ctx", split_axis=1, concat_axis=2, tiled=True)
     mixed = after_reading(read, count)
     mixed = mixed.reshape(mixed.shape[0], mixed.shape[1], -1)
-    return jnp.einsum(
-        "btw,wv->btv",
-        mixed,
-        lax.all_gather(out_weight, "batch", axis=0, tiled=True),
-        preferred_element_type=jnp.float32,
+    return summed_both_ways(
+        out_weight,
+        "batch",
+        0,
+        lambda own_block, offset: jnp.einsum(
+            "btw,wv->btv",
+            lax.dynamic_slice_in_dim(mixed, offset, own_block.shape[0], axis=2),
+            own_block,
+            preferred_element_type=jnp.float32,
+        ),
     ).astype(jnp.bfloat16)
 
 

time: 331 us -> 551 us (1.66)
  waiting for transfers between devices: 166 us -> 458 us
  blocking collectives: 81.2 us -> 0 us
  between operations: 13.5 us -> 0.11 us
  starting transfers between devices: 10 us -> 22.4 us
  matrix products: 17.8 us -> 23.5 us
    ppermute x0 -> x3, waiting for transfers between devices: none -> 360 us  [the longest x2 283 us: summed_both_ways(): from_left = lax.ppermute(from_left, axis, ahead)]
    all_gather x1 -> x0, waiting for transfers between devices: 121 us -> none  [shards(): lax.all_gather(out_weight, 'batch', axis=0, tiled=True)]
    all_to_all x2 -> x0, blocking collectives: 81.2 us -> none  [the longest x1 52.2 us: shards(): lax.all_to_all(head_read, 'ctx', split_axis=1, concat_axis=2, tiled=True)]
    all_to_all x0 -> x2, waiting for transfers between devices: none -> 74 us  [the longest x1 49 us: shards(): lax.all_to_all(head_read, 'ctx', split_axis=1, concat_axis=2, tiled=True)]
    all_to_all x1, waiting for transfers between devices: 19.3 us -> 0.01 us  [shards(): lax.all_to_all(contents, 'ctx', split_axis=2, concat_axis=1, tiled=True)]
    all_to_all x0 -> x2, starting transfers between devices: none -> 8.44 us  [the longest x1 4.88 us: shards(): lax.all_to_all(head_read, 'ctx', split_axis=1, concat_axis=2, tiled=True)]
    dot_general x1 -> x4, matrix products: 14 us -> 19.7 us  [shards(): jnp.einsum('btw,wv->btv', lax.dynamic_slice_in_dim(mixed, offset, own_blo...]
    ppermute x0 -> x3, starting transfers between devices: none -> 5.52 us  [the longest x2 4.03 us: summed_both_ways(): from_left = lax.ppermute(from_left, axis, ahead)]
  transfers between devices with their start and end apart: 3 -> 7, of which waited for: 3 -> 6; matrix products, arithmetic and copies ran while one was open for 14% -> 11% of each run, Pallas kernels for 0% -> 0%
where the time goes in v1:
time: 551 us; the launch traced here: 550 us
  waiting for transfers between devices  458 us (83%)
  local copies, waits for them, and re-layouts  31.4 us (6%)
  matrix products  23.5 us (4%)
  starting transfers between devices  22.4 us (4%)
  other arithmetic  14.5 us (3%)
    ppermute x2, waiting for transfers between devices, summed_both_ways(): from_left = lax.ppermute(from_left, axis, ahead)  283 us
    ppermute x1, waiting for transfers between devices, summed_both_ways(): from_right = lax.ppermute(from_right, axis, backward)  76.5 us
    all_to_all x1, waiting for transfers between devices, shards(): lax.all_to_all(head_read, 'ctx', split_axis=1, concat_axis=2, tiled=True)  49 us
    all_to_all x1, waiting for transfers between devices, shards(): lax.all_to_all(key_feature, 'ctx', split_axis=2, concat_axis=1, tiled=True)  25 us
    all_to_all x1, waiting for transfers between devices, shards(): lax.all_to_all(query_feature, 'ctx', split_axis=2, concat_axis=1, tiled=T...  24.4 us
    dot_general x4, matrix products, shards(): jnp.einsum('btw,wv->btv', lax.dynamic_slice_in_dim(mixed, offset, own_blo...  19.7 us
    unnamed x9, local copies, waits for them, and re-layouts  12.5 us
  transfers between devices with their start and end apart: 7, of which 6 were waited for; matrix products, arithmetic and copies ran while one was open for 11% of the time, Pallas kernels for 0%

profile of v1, /device:TPU:0, one launch (start us, length us, event | category | flops | bytes accessed | tf_op | source)
XLA Modules:
  0.0 549.9 jit_solution(6972778825171388220)
XLA Ops:
  0.0 3.0 collective-permute-start.1
  3.0 3.4 fusion.11
  6.4 4.9 all-to-all-start.2
  11.3 2.2 fusion.10
  13.5 24.4 %all-to-all-done.2 = bf16[1,128,64,64]{1,3,0,2:T(8,128)(2,1)S(1)} async-done(((bf16[1,128,64,64]{1,3,0,2:T(8,128)(2,1)}), bf16[1,128,64,64]{1,3,0,2:T(8,128)(2,1)S(1)}, u32[]{:S(2)}, u32[]{:S(2)}) %all-to-all-start.2) | async-done | bytes 1048608 | tf_op jit(solution)/shard_map/all_to_all | solution.py:47
  37.8 3.6 all-to-all-start
  41.4 1.5 collective-permute-start
  42.9 25.0 %all-to-all-done = bf16[1,128,64,64]{1,3,0,2:T(8,128)(2,1)S(1)} async-done(((bf16[1,128,64,64]{1,3,0,2:T(8,128)(2,1)}), bf16[1,128,64,64]{1,3,0,2:T(8,128)(2,1)S(1)}, u32[]{:S(2)}, u32[]{:S(2)}) %all-to-all-start) | async-done | bytes 1048608 | tf_op jit(solution)/shard_map/all_to_all | solution.py:48
  67.9 3.6 all-to-all-start.1
  71.4 114.1 %collective-permute-done.1 = bf16[1024,4096]{1,0:T(8,128)(2,1)} collective-permute-done((bf16[1024,4096]{1,0:T(8,128)(2,1)}, bf16[1024,4096]{1,0:T(8,128)(2,1)}, u32[]{:S(2)}, u32[]{:S(2)}) %collective-permute-start.1) | collective-permute-done | bytes 8388640 | tf_op jit(solution)/shard_map/ppermute | solution.py:15
  186.6 1.7 copy.48
  188.3 1.5 reshape.81
  189.8 1.7 copy.50
  191.5 2.3 reshape.79
  193.8 1.7 copy.49
  195.5 2.4 reshape.80
  197.9 1.4 convert_reduce_fusion
  199.9 3.2 bitcast_divide_fusion
  203.1 3.8 copy.35
  206.9 7.2 %reshape.88 = f32[8,1,65536]{2,1,0:T(1,128)} reshape(f32[1024,1,8,64]{3,2,1,0:T(8,128)} %bitcast.83) | data formatting | bytes 4194304
  214.2 4.9 all-to-all-start.3
  219.0 49.0 %all-to-all-done.3 = f32[8,1,65536]{2,1,0:T(1,128)S(1)} async-done(((f32[8,1,65536]{2,1,0:T(1,128)}), f32[8,1,65536]{2,1,0:T(1,128)S(1)}, u32[]{:S(2)}, u32[]{:S(2)}) %all-to-all-start.3) | async-done | bytes 2097184 | tf_op jit(solution)/shard_map/all_to_all | solution.py:57
  268.1 1.4 copy-done
  269.9 7.2 %reduce.2 = f32[8,65536]{1,0:T(8,128)S(1)} reduce(f32[8,1,65536]{2,1,0:T(1,128)} %copy-done, f32[]{:T(128)} %broadcast.29), dimensions={1}, to_apply=%all_to_all.49.reduce_sub_computation | reduce | bytes 4194308 | tf_op jit(solution)/shard_map/all_to_all | solution.py:57
  277.2 3.6 reshape.89
  280.8 3.0 copy.36
  284.6 4.7 fusion.16
  289.3 76.5 %collective-permute-done = bf16[1024,4096]{1,0:T(8,128)(2,1)} collective-permute-done((bf16[1024,4096]{1,0:T(8,128)(2,1)}, bf16[1024,4096]{1,0:T(8,128)(2,1)}, u32[]{:S(2)}, u32[]{:S(2)}) %collective-permute-start) | collective-permute-done | bytes 8388640 | tf_op jit(solution)/shard_map/ppermute | solution.py:17
  365.8 4.7 convolution_add_fusion.2
  370.6 4.7 convolution_add_fusion.1
  375.2 169.0 %collective-permute-done.2 = bf16[1024,4096]{1,0:T(8,128)(2,1)} collective-permute-done((bf16[1024,4096]{1,0:T(8,128)(2,1)}, bf16[1024,4096]{1,0:T(8,128)(2,1)}, u32[]{:S(2)}, u32[]{:S(2)}) %collective-permute-start.2) | collective-permute-done | bytes 8388640 | tf_op jit(solution)/shard_map/ppermute | solution.py:15
  544.2 5.6 %fusion.1 = bf16[1,128,4096]{2,1,0:T(8,128)(2,1)} fusion(f32[128,4096]{1,0:T(8,128)S(1)} %convolution_add_fusion.1, bf16[1024,4096]{1,0:T(8,128)(2,1)} %collective-permute-done.2, bf16[1,128,4096]{1,2,0:T(8,128)(2,1)S(1)} %bitcast.90, s32[]{:T(128)S(6)} %select_n.42), kind=kOutput, calls=%fused_computation.6 | convolution fusion | flops 1074790400 | bytes 11796484 | tf_op jit(solution)/shard_map/btw,wv->btv/dot_general | solution.py:64
  (14 shorter events, 2.9 us)
Async XLA Ops:
  0.0 11.3 %copy-start.1 = (bf16[1,128,64,64]{1,3,2,0:T(8,128)(2,1)S(1)}, bf16[1,128,64,64]{1,3,2,0:T(8,128)(2,1)}, u32[]{:S(2)}) copy-start(bf16[1,128,64,64]{1,3,2,0:T(8,128)(2,1)} %param.5) | copy-start | bytes 3145732
  0.0 185.5 %collective-permute-start.1 = (bf16[1024,4096]{1,0:T(8,128)(2,1)}, bf16[1024,4096]{1,0:T(8,128)(2,1)}, u32[]{:S(2)}, u32[]{:S(2)}) collective-permute-start(bf16[1024,4096]{1,0:T(8,128)(2,1)} %param.7), channel_id=1, source_target_pairs={{0,8},{8,16},{16,24},{24,0},{1,9},{9,17},{17,25},{25,1},{2,10},{10... | collective-permute-start | bytes 25165832 | tf_op jit(solution)/shard_map/ppermute | solution.py:15
  6.4 31.4 %all-to-all-start.2 = ((bf16[1,128,64,64]{1,3,0,2:T(8,128)(2,1)}), bf16[1,128,64,64]{1,3,0,2:T(8,128)(2,1)S(1)}, u32[]{:S(2)}, u32[]{:S(2)}) async-start(bf16[1,128,64,64]{1,3,0,2:T(8,128)(2,1)} %fusion.11), calls=%async_computation.2 | async-start | bytes 2097152 | tf_op jit(solution)/shard_map/all_to_all | solution.py:47
  37.8 30.1 %all-to-all-start = ((bf16[1,128,64,64]{1,3,0,2:T(8,128)(2,1)}), bf16[1,128,64,64]{1,3,0,2:T(8,128)(2,1)S(1)}, u32[]{:S(2)}, u32[]{:S(2)}) async-start(bf16[1,128,64,64]{1,3,0,2:T(8,128)(2,1)} %fusion.10), calls=%async_computation | async-start | bytes 2097152 | tf_op jit(solution)/shard_map/all_to_all | solution.py:48
  41.4 324.4 %collective-permute-start = (bf16[1024,4096]{1,0:T(8,128)(2,1)}, bf16[1024,4096]{1,0:T(8,128)(2,1)}, u32[]{:S(2)}, u32[]{:S(2)}) collective-permute-start(bf16[1024,4096]{1,0:T(8,128)(2,1)} %param.7), channel_id=1, source_target_pairs={{0,24},{8,0},{16,8},{24,16},{1,25},{9,1},{17,9},{25,17},{2,26},{10... | collective-permute-start | bytes 25165832 | tf_op jit(solution)/shard_map/ppermute | solution.py:17
  67.9 125.9 %all-to-all-start.1 = ((bf16[1,128,64,64]{1,3,0,2:T(8,128)(2,1)}), bf16[1,128,64,64]{1,3,0,2:T(8,128)(2,1)S(1)}, u32[]{:S(2)}, u32[]{:S(2)}) async-start(bf16[1,128,64,64]{1,3,0,2:T(8,128)(2,1)} %bitcast.98), calls=%async_computation.1 | async-start | bytes 2097152 | tf_op jit(solution)/shard_map/all_to_all | solution.py:49
  185.5 358.7 %collective-permute-start.2 = (bf16[1024,4096]{1,0:T(8,128)(2,1)}, bf16[1024,4096]{1,0:T(8,128)(2,1)}, u32[]{:S(2)}, u32[]{:S(2)}) collective-permute-start(bf16[1024,4096]{1,0:T(8,128)(2,1)} %collective-permute-done.1), channel_id=1, source_target_pairs={{0,8},{8,16},{16,24},{24,0},{1,9},{9,17},{17,25},{25,1},{2,10},{10... | collective-permute-start | bytes 25165832 | tf_op jit(solution)/shard_map/ppermute | solution.py:15
  195.5 4.4 copy-start.2
  214.2 53.9 %all-to-all-start.3 = ((f32[8,1,65536]{2,1,0:T(1,128)}), f32[8,1,65536]{2,1,0:T(1,128)S(1)}, u32[]{:S(2)}, u32[]{:S(2)}) async-start(f32[8,1,65536]{2,1,0:T(1,128)} %reshape.88), calls=%async_computation.3 | async-start | bytes 4194304 | tf_op jit(solution)/shard_map/all_to_all | solution.py:57
  268.1 1.4 copy-start
